TPU v7x, 32 devices: a whole 2x2x4 slice. The times are simulated.
32 devices in a mesh: parts: 2 (over y), seq: 16 (over z, x, core).
Axes of the slice: x: 2, y: 2, z: 4, core: 2. Of those that a mesh axis runs over, the one named last changes fastest.
Arguments:
- queries: float32 [4096, 4096], P(('parts', 'seq')), parts along dimension 0, may hold values from -11 to 11
- visual_keys: float32 [4096, 512], P(('parts', 'seq')), parts along dimension 0, may hold values from -4 to 4
- visual_value_rows: float32 [4096, 512], P(('parts', 'seq')), parts along dimension 0, may hold values from -6 to 6
- output_gradient: float32 [4096, 4096], P(('parts', 'seq')), parts along dimension 0, may hold values from -6 to 6
- query_head_gate: float32 [32], replicated, may hold values from 0.3 to 2
- window_lists: int32 [2, 6], P('parts'), parts along dimension 0, may hold values from 0 to 15, as said below
- block_place: int32 [32], P('parts'), parts along dimension 0, may hold values from 0 to 15, each once
Outputs:
- output: float32 [4096, 4096], P(('parts', 'seq')), parts along dimension 0
- grad_queries: float32 [4096, 4096], P(('parts', 'seq')), parts along dimension 0
- grad_keys: float32 [4096, 512], P(('parts', 'seq')), parts along dimension 0
- grad_values: float32 [4096, 512], P(('parts', 'seq')), parts along dimension 0
There are 2 independent parts, one for each index of `parts`. A program takes and returns all parts, laid end to end along the dimension named above; an argument that names none is the same for every part. Nothing has to cross between parts.
Inputs may be any that keep to these rules, and one draw needn't show every extreme that they name: `window_lists`: each row names 6 different visual blocks.
All inputs are finite; a program needn't handle non-finite values.
Results may differ from a plain program's by a relative error of at most 0.0003.
Values sent between devices are 32-bit elements; how exact they have to be, the bound alone decides.
No kernel may reach another device: no remote copies, remote signals or barrier semaphores. Data moves between devices by JAX's collectives and lax.ppermute only.
A program may use at most 128 MiB of HBM per device.

v0:
```python
import functools

import jax
import jax.numpy as jnp
from jax import lax
from jax.experimental import pallas as pl
from jax.experimental.pallas import tpu as pltpu
from jax.sharding import PartitionSpec as P

F = 128
BLOCK_TOKENS = 128
WINDOW_ROWS = 2048
CORES = 2
HEADS = 8
CHUNK = 128
LN2 = 0.6931471805599453
LOG2E = 1.4426950408889634
BF = jnp.bfloat16
F32 = jnp.float32


def split(x):
    high = x.astype(BF)
    return high, (x - high.astype(F32)).astype(BF)


def dot(a, b):
    return lax.dot_general(a, b, (((1,), (0,)), ((), ())), preferred_element_type=F32)


def kernel(n_in, groups, steps, keys, core_ref, gate_ref, qo_ref, qp_ref, go_ref, gp_ref, *rest):
    kv_in = rest[:n_in]
    oo_ref, op_ref, do_ref, dp_ref, dkv_ref = rest[n_in : n_in + 5]
    kv, kk, vv, kt, vt, s_ref, ph, plo, dh, dlo, dka, dva, sem = rest[n_in + 5 :]
    g, side, p = pl.program_id(0), pl.program_id(1), pl.program_id(2)
    inv_root = F ** (-0.5)
    half = groups * F

    @pl.when((g == 0) & (side == 0) & (p == 0))
    def _():
        copies, at = [], 0
        for i, src in enumerate(kv_in):
            rows = src.shape[0]
            copies.append(pltpu.make_async_copy(src, kv.at[pl.ds(at, rows)], sem.at[i]))
            at += rows
        for c in copies:
            c.start()
        for c in copies:
            c.wait()

    @pl.when((side == 0) & (p == 0))
    def _():
        for off, pack, tr in ((0, kk, kt), (half, vv, vt)):
            x = kv[:, pl.ds(pl.multiple_of(off + g * F, F), F)]
            high, low = split(x)
            pack[:, 0:F] = high
            pack[:, F : 2 * F] = low
            pack[:, 2 * F : 3 * F] = high
            pack[:, 3 * F : 4 * F] = low
            high, low = split(x.T)
            tr[0:F, :] = high
            tr[F : 2 * F, :] = low
        dka[...] = jnp.zeros_like(dka)
        dva[...] = jnp.zeros_like(dva)

    def pack_rows(own, other, scale):
        x = jnp.where(side == 0, own[...], other[...])
        xs = [x[:, h * F : (h + 1) * F] * scale(h) for h in range(HEADS)]
        rh, rl = split(jnp.concatenate(xs, axis=0))
        cols = jnp.concatenate([y.T for y in xs], axis=1)
        ch, cl = split(cols)
        return jnp.concatenate([rh, rl], axis=1), jnp.concatenate([ch, ch, cl, cl], axis=0), cols

    base = ((core_ref[0] * groups + g) * steps + p) * HEADS
    gates = [gate_ref[base + h] for h in range(HEADS)]
    qr, qc, _ = pack_rows(qo_ref, qp_ref, lambda h: inv_root * LOG2E)
    ar, ac, acols = pack_rows(go_ref, gp_ref, lambda h: gates[h])

    def put(own, other, values):
        @pl.when(side == 0)
        def _():
            for h, y in enumerate(values):
                own[:, h * F : (h + 1) * F] = y

        @pl.when(side != 0)
        def _():
            for h, y in enumerate(values):
                other[:, h * F : (h + 1) * F] = y

    tiles = [slice(c, c + CHUNK) for c in range(0, keys, CHUNK)]
    m = None
    for t in tiles:
        s = dot(kk[t, :], qc)
        s_ref[t, :] = s
        mc = jnp.max(s, axis=0, keepdims=True)
        m = mc if m is None else jnp.maximum(m, mc)
    l = None
    for t in tiles:
        e = jnp.exp2(s_ref[t, :] - m)
        s_ref[t, :] = e
        lc = jnp.sum(e, axis=0, keepdims=True)
        l = lc if l is None else l + lc
    inv = 1.0 / l
    for t in tiles:
        w = s_ref[t, :] * inv
        s_ref[t, :] = w
        ph[t, :], plo[t, :] = split(w)
    o2 = dot(vt[...], ph[...])
    ot = o2[0:F, :] + o2[F : 2 * F, :] + dot(vt[0:F, :], plo[...])
    delta = jnp.sum(ot * acols, axis=0, keepdims=True)
    put(oo_ref, op_ref, [ot[:, h * F : (h + 1) * F].T * gates[h] for h in range(HEADS)])
    for t in tiles:
        dva[t, :] += dot(ph[t, :], ar) + dot(plo[t, :], ar)
    for t in tiles:
        ds = s_ref[t, :] * (dot(vv[t, :], ac) - delta)
        dh[t, :], dlo[t, :] = split(ds)
    for t in tiles:
        dka[t, :] += dot(dh[t, :], qr) + dot(dlo[t, :], qr)
    d2 = dot(kt[...], dh[...])
    dt = (d2[0:F, :] + d2[F : 2 * F, :] + dot(kt[0:F, :], dlo[...])) * inv_root
    put(do_ref, dp_ref, [dt[:, h * F : (h + 1) * F].T for h in range(HEADS)])

    @pl.when((side == pl.num_programs(1) - 1) & (p == steps - 1))
    def _():
        col = pl.multiple_of(g * F, F)
        dkv_ref[:, pl.ds(col, F)] = (dka[:, 0:F] + dka[:, F : 2 * F]) * LN2
        dkv_ref[:, pl.ds(pl.multiple_of(half + col, F), F)] = dva[:, 0:F] + dva[:, F : 2 * F]


def attend(core, gate, q_own, q_other, g_own, g_other, kv_in):
    rows = q_own.shape[0]
    width = kv_in[0].shape[1]
    groups = width // F // 2
    steps = q_other.shape[1] // F // groups // HEADS
    n_in = len(kv_in)
    keys = sum(x.shape[0] for x in kv_in)
    n = HEADS * rows
    blocks = groups * steps

    def own(g, side, p, c):
        return 0, c[0] * blocks + g * steps + jnp.where(side == 0, p, steps - 1)

    def other(g, side, p, c):
        return 0, g * steps + jnp.where(side == 0, 0, p)

    own_block = pl.BlockSpec((rows, HEADS * F), own)
    other_block = pl.BlockSpec((rows, HEADS * F), other)
    anywhere = pl.BlockSpec(memory_space=pl.ANY)
    full = jax.ShapeDtypeStruct(q_own.shape, F32)
    part = jax.ShapeDtypeStruct(q_other.shape, F32)
    spec = pltpu.PrefetchScalarGridSpec(
        num_scalar_prefetch=1,
        grid=(groups, 2, steps),
        in_specs=[pl.BlockSpec(memory_space=pltpu.SMEM), own_block, other_block, own_block, other_block]
        + [anywhere] * n_in,
        out_specs=[
            own_block,
            other_block,
            own_block,
            other_block,
            pl.BlockSpec((keys, width), lambda g, side, p, c: (0, 0)),
        ],
        scratch_shapes=[
            pltpu.VMEM((keys, width), F32),
            pltpu.VMEM((keys, 4 * F), BF),
            pltpu.VMEM((keys, 4 * F), BF),
            pltpu.VMEM((2 * F, keys), BF),
            pltpu.VMEM((2 * F, keys), BF),
            pltpu.VMEM((keys, n), F32),
            pltpu.VMEM((keys, n), BF),
            pltpu.VMEM((keys, n), BF),
            pltpu.VMEM((keys, n), BF),
            pltpu.VMEM((keys, n), BF),
            pltpu.VMEM((keys, 2 * F), F32),
            pltpu.VMEM((keys, 2 * F), F32),
            pltpu.SemaphoreType.DMA((n_in,)),
        ],
    )
    return pl.pallas_call(
        functools.partial(kernel, n_in, groups, steps, keys),
        out_shape=[full, part, full, part, jax.ShapeDtypeStruct((keys, width), F32)],
        grid_spec=spec,
        compiler_params=pltpu.CompilerParams(
            dimension_semantics=("arbitrary",) * 3, vmem_limit_bytes=56 << 20
        ),
        cost_estimate=pl.CostEstimate(
            flops=48 * rows * q_other.shape[1] * keys,
            bytes_accessed=32 * rows * q_other.shape[1],
            transcendentals=2 * rows * q_other.shape[1] // F * keys,
        ),
        name="attend",
    )(core, gate, q_own, q_other, g_own, g_other, *kv_in)


def ring_tables(devices, members):
    chips = members // CORES
    order = list(range(0, chips, 2)) + [c for c in range(chips - 1, 0, -1) if c % 2]
    right, left, pair = [], [], []
    for base in range(0, devices, members):
        for at, c in enumerate(order):
            after = order[(at + 1) % chips]
            for core in range(CORES):
                a, b = base + CORES * c + core, base + CORES * after + core
                right.append((a, b))
                left.append((b, a))
                pair.append((a, base + CORES * c + 1 - core))
    return chips, right, left, pair


def local(queries, visual_keys, visual_value_rows, output_gradient, query_head_gate, window_lists, block_place):
    row_count, q_width = queries.shape
    width = visual_keys.shape[1]
    list_len = window_lists.shape[1]
    devices = lax.axis_size("seq")
    members = WINDOW_ROWS // row_count
    windows = devices // members
    blocks_here = visual_keys.shape[0] // BLOCK_TOKENS
    positions = devices * blocks_here
    chips, right, left, pair = ring_tables(devices, members)
    piece = BLOCK_TOKENS // chips
    half_width, q_half = width // CORES, q_width // CORES
    far = chips // 2
    index = lax.axis_index("seq")
    core = index % CORES

    def shift(x, table):
        return lax.ppermute(x, "seq", table)

    mine = lax.dynamic_index_in_dim(window_lists, index // members, 0, keepdims=False)
    wanted = jnp.take(block_place, mine, axis=0)

    def theirs(x):
        return shift(lax.dynamic_slice_in_dim(x, (1 - core) * q_half, q_half, 1), pair)

    def by_core(x):
        x = x.reshape(blocks_here, chips, piece, CORES, half_width)
        return x.transpose(0, 1, 3, 2, 4)

    x = jnp.concatenate([by_core(visual_keys), by_core(visual_value_rows)], axis=-1)
    x = x.reshape(blocks_here, members, piece, width)
    x = jnp.tile(x, (1, windows, 1, 1))
    x = lax.all_to_all(x, "seq", split_axis=1, concat_axis=0, tiled=True)
    q_other, g_other = theirs(queries), theirs(output_gradient)
    x = jnp.take(x.reshape(positions, piece, width), wanted, axis=0).reshape(list_len * piece, width)

    n = x.shape[0]
    cut = n // 2
    rights, lefts = [], []
    r = l = x
    for step in range(1, far + 1):
        if step == far:
            r, l = r[:cut], l[cut:]
        r, l = shift(r, right), shift(l, left)
        rights.append(r)
        lefts.append(l)
    chunks = [x] + rights + lefts
    gate = jnp.tanh(query_head_gate)
    out_own, out_other, dq_own, dq_other, dkv = attend(
        core.reshape(1), gate, queries, q_other, output_gradient, g_other, chunks
    )
    parts, at = [], 0
    for c in chunks:
        parts.append(dkv[at : at + c.shape[0]])
        at += c.shape[0]
    rights, lefts = parts[1 : 1 + far], parts[1 + far :]
    r, l = shift(rights[-1], left), shift(lefts[-1], right)
    for step in range(far - 1, 0, -1):
        a, b = rights[step - 1], lefts[step - 1]
        if step == far - 1:
            a = jnp.concatenate([a[:cut] + r, a[cut:]], axis=0)
            b = jnp.concatenate([b[:cut], b[cut:] + l], axis=0)
        else:
            a, b = a + r, b + l
        r, l = shift(a, left), shift(b, right)
    out_back, dq_back = shift(out_other, pair), shift(dq_other, pair)
    total = (parts[0] + r + l).reshape(list_len, piece, width)
    hit = wanted[None, :] == jnp.arange(positions, dtype=jnp.int32)[:, None]
    slot = jnp.argmax(hit, axis=1)
    sent = jnp.where(jnp.any(hit, axis=1)[:, None, None], jnp.take(total, slot, axis=0), 0.0)
    back = lax.all_to_all(
        sent.reshape(devices, blocks_here, piece, width), "seq", split_axis=0, concat_axis=0, tiled=True
    ).reshape(windows, chips, CORES, blocks_here, piece, width)
    back = back[0] if windows == 1 else jnp.sum(back, axis=0)

    def by_rows(x):
        return x.transpose(2, 0, 3, 1, 4).reshape(blocks_here * BLOCK_TOKENS, width)

    def whole(x, y):
        return lax.dynamic_update_slice_in_dim(x, y, (1 - core) * q_half, 1)

    return (
        whole(out_own, out_back),
        whole(dq_own, dq_back),
        by_rows(back[..., :half_width]),
        by_rows(back[..., half_width:]),
    )


def solution(mesh):
    rows = P(("parts", "seq"), None)
    return jax.shard_map(
        local,
        mesh=mesh,
        in_specs=(rows, rows, rows, rows, P(), P("parts", None), P("parts")),
        out_specs=(rows, rows, rows, rows),
        check_vma=False,
    )
```

profile of v0, /device:TPU:0, one launch (start us, length us, event | category | flops | bytes accessed | tf_op | source)
XLA Modules:
  0.0 141.3 jit_solution(701559566999728754)
XLA Ops:
  0.7 1.4 constant_dynamic-slice_fusion.1
  2.0 0.6 collective-permute-start
  3.3 0.9 copy.22
  4.1 7.0 %all-to-all-start = ((f32[1,16,16,512]{3,2,0,1:T(8,128)}), f32[1,16,16,512]{3,2,0,1:T(8,128)S(1)}, u32[]{:S(2)}, u32[]{:S(2)}) async-start(f32[1,16,16,512]{3,2,0,1:T(8,128)} %bitcast.7), calls=%async_computation | async-start | bytes 1048576 | tf_op jit(solution)/shard_map/all_to_all | solution.py:242
  11.2 1.3 constant_dynamic-slice_fusion
  12.5 0.5 collective-permute-start.1
  13.0 0.6 gather_fusion
  13.8 11.6 %all-to-all-done = f32[1,16,16,512]{3,2,0,1:T(8,128)S(1)} async-done(((f32[1,16,16,512]{3,2,0,1:T(8,128)}), f32[1,16,16,512]{3,2,0,1:T(8,128)S(1)}, u32[]{:S(2)}, u32[]{:S(2)}) %all-to-all-start) | async-done | bytes 524320 | tf_op jit(solution)/shard_map/all_to_all | solution.py:242
  25.4 0.6 gather_fusion.1
  26.1 1.2 collective-permute-start.2
  27.3 0.9 collective-permute-start.6
  28.2 4.9 %collective-permute-done.2.rest_1_ = f32[96,512]{1,0:T(8,128)S(1)} collective-permute-done((f32[96,512]{1,0:T(8,128)S(1)}, f32[96,512]{1,0:T(8,128)S(1)}, u32[]{:S(2)}, u32[]{:S(2)}) %collective-permute-start.2) | collective-permute-done | bytes 196640 | tf_op jit(solution)/shard_map/ppermute | solution.py:227
  33.1 1.7 %collective-permute-start.3 = (f32[96,512]{1,0:T(8,128)S(1)}, f32[96,512]{1,0:T(8,128)S(1)}, u32[]{:S(2)}, u32[]{:S(2)}) collective-permute-start(f32[96,512]{1,0:T(8,128)S(1)} %collective-permute-done.2.rest_1_), channel_id=1, source_target_pairs={{0,4},{1,5},{4,8},{5,9},{8,12},{9,13},{12,14},{13,15},{14,10},{15,... | collective-permute-start | bytes 589832 | tf_op jit(solution)/shard_map/ppermute | solution.py:227
  35.1 4.4 %collective-permute-done.3.rest_2_ = f32[96,512]{1,0:T(8,128)S(1)} collective-permute-done((f32[96,512]{1,0:T(8,128)S(1)}, f32[96,512]{1,0:T(8,128)S(1)}, u32[]{:S(2)}, u32[]{:S(2)}) %collective-permute-start.3) | collective-permute-done | bytes 196640 | tf_op jit(solution)/shard_map/ppermute | solution.py:227
  39.5 2.0 %collective-permute-start.4 = (f32[96,512]{1,0:T(8,128)S(1)}, f32[96,512]{1,0:T(8,128)S(1)}, u32[]{:S(2)}, u32[]{:S(2)}) collective-permute-start(f32[96,512]{1,0:T(8,128)S(1)} %collective-permute-done.3.rest_2_), channel_id=1, source_target_pairs={{0,4},{1,5},{4,8},{5,9},{8,12},{9,13},{12,14},{13,15},{14,10},{15,... | collective-permute-start | bytes 589832 | tf_op jit(solution)/shard_map/ppermute | solution.py:227
  41.6 4.0 %collective-permute-done.4.rest_3_ = f32[96,512]{1,0:T(8,128)S(1)} collective-permute-done((f32[96,512]{1,0:T(8,128)S(1)}, f32[96,512]{1,0:T(8,128)S(1)}, u32[]{:S(2)}, u32[]{:S(2)}) %collective-permute-start.4) | collective-permute-done | bytes 196640 | tf_op jit(solution)/shard_map/ppermute | solution.py:227
  45.6 1.8 %collective-permute-start.5 = (f32[48,512]{1,0:T(8,128)S(1)}, f32[48,512]{1,0:T(8,128)S(1)}, u32[]{:S(2)}, u32[]{:S(2)}) collective-permute-start(f32[48,512]{1,0:T(8,128)S(1)} %slice.72), channel_id=1, source_target_pairs={{0,4},{1,5},{4,8},{5,9},{8,12},{9,13},{12,14},{13,15},{14,10},{15,... | collective-permute-start | bytes 294920 | tf_op jit(solution)/shard_map/ppermute | solution.py:227
  47.5 0.3 collective-permute-start.9
  47.8 0.6 tanh.3.gate_ref
  48.4 1.9 %collective-permute-done.5.rest_4_ = f32[48,512]{1,0:T(8,128)S(1)} collective-permute-done((f32[48,512]{1,0:T(8,128)S(1)}, f32[48,512]{1,0:T(8,128)S(1)}, u32[]{:S(2)}, u32[]{:S(2)}) %collective-permute-start.5) | collective-permute-done | bytes 98336 | tf_op jit(solution)/shard_map/ppermute | solution.py:227
  50.3 1.9 %collective-permute-done.9.rest_8_ = f32[48,512]{1,0:T(8,128)S(1)} collective-permute-done((f32[48,512]{1,0:T(8,128)S(1)}, f32[48,512]{1,0:T(8,128)S(1)}, u32[]{:S(2)}, u32[]{:S(2)}) %collective-permute-start.9) | collective-permute-done | bytes 98336 | tf_op jit(solution)/shard_map/ppermute | solution.py:227
  52.2 0.6 copy-done.12
  52.8 34.1 %attend.1 = (f32[128,4096]{1,0:T(8,128)}, f32[128,2048]{1,0:T(8,128)}, f32[128,4096]{1,0:T(8,128)}, f32[128,2048]{1,0:T(8,128)}, f32[768,512]{1,0:T(8,128)}) custom-call(s32[1]{0:T(128)} %bitcast.core_ref, f32[32]{0:T(128)} %tanh.3.gate_ref, f32[128,4096]{1,0:T(8,128)} %qo_ref.1, f32[128,2048]{1,0:T(8,128)} %collective-permute-done.qp_ref, ...), custom_call_target="tpu_custom_call" | custom-call | flops 9663676416 | bytes 8388608 | tf_op jit(solution)/shard_map/attend/pallas_call | solution.py:179
  86.9 1.0 slice.57
  88.1 0.6 iota_reduce_fusion
  88.7 4.3 %collective-permute-done.12 = f32[48,512]{1,0:T(8,128)S(1)} collective-permute-done((f32[48,512]{1,0:T(8,128)S(1)}, f32[48,512]{1,0:T(8,128)S(1)}, u32[]{:S(2)}, u32[]{:S(2)}) %collective-permute-start.12) | collective-permute-done | bytes 98336 | tf_op jit(solution)/shard_map/ppermute | solution.py:227
  93.1 1.1 slice_add_fusion.5
  94.1 0.3 collective-permute-start.16
  94.5 1.8 %collective-permute-start.13 = (f32[96,512]{1,0:T(8,128)S(1)}, f32[96,512]{1,0:T(8,128)S(1)}, u32[]{:S(2)}, u32[]{:S(2)}) collective-permute-start(f32[96,512]{1,0:T(8,128)S(1)} %pad_maximum_fusion.1), channel_id=1, source_target_pairs={{4,0},{5,1},{8,4},{9,5},{12,8},{13,9},{14,12},{15,13},{10,14},{11,... | collective-permute-start | bytes 589832 | tf_op jit(solution)/shard_map/ppermute | solution.py:227
  96.3 3.4 %collective-permute-done.16 = f32[48,512]{1,0:T(8,128)S(1)} collective-permute-done((f32[48,512]{1,0:T(8,128)S(1)}, f32[48,512]{1,0:T(8,128)S(1)}, u32[]{:S(2)}, u32[]{:S(2)}) %collective-permute-start.16) | collective-permute-done | bytes 98336 | tf_op jit(solution)/shard_map/ppermute | solution.py:227
  99.7 0.9 slice_add_fusion.4
  100.7 0.4 collective-permute-start.17
  101.4 1.5 %collective-permute-start.14 = (f32[96,512]{1,0:T(8,128)S(1)}, f32[96,512]{1,0:T(8,128)S(1)}, u32[]{:S(2)}, u32[]{:S(2)}) collective-permute-start(f32[96,512]{1,0:T(8,128)S(1)} %slice_add_fusion.2), channel_id=1, source_target_pairs={{4,0},{5,1},{8,4},{9,5},{12,8},{13,9},{14,12},{15,13},{10,14},{11,... | collective-permute-start | bytes 589832 | tf_op jit(solution)/shard_map/ppermute | solution.py:227
  102.8 4.5 %collective-permute-done.17 = f32[96,512]{1,0:T(8,128)S(1)} collective-permute-done((f32[96,512]{1,0:T(8,128)S(1)}, f32[96,512]{1,0:T(8,128)S(1)}, u32[]{:S(2)}, u32[]{:S(2)}) %collective-permute-start.17) | collective-permute-done | bytes 196640 | tf_op jit(solution)/shard_map/ppermute | solution.py:227
  107.5 0.6 collective-permute-start.18
  108.2 1.5 %collective-permute-start.15 = (f32[96,512]{1,0:T(8,128)S(1)}, f32[96,512]{1,0:T(8,128)S(1)}, u32[]{:S(2)}, u32[]{:S(2)}) collective-permute-start(f32[96,512]{1,0:T(8,128)S(1)} %get-tuple-element.16), channel_id=1, source_target_pairs={{4,0},{5,1},{8,4},{9,5},{12,8},{13,9},{14,12},{15,13},{10,14},{11,... | collective-permute-start | bytes 589832 | tf_op jit(solution)/shard_map/ppermute | solution.py:227
  109.6 3.7 %collective-permute-done.18 = f32[96,512]{1,0:T(8,128)S(1)} collective-permute-done((f32[96,512]{1,0:T(8,128)S(1)}, f32[96,512]{1,0:T(8,128)S(1)}, u32[]{:S(2)}, u32[]{:S(2)}) %collective-permute-start.18) | collective-permute-done | bytes 196640 | tf_op jit(solution)/shard_map/ppermute | solution.py:227
  113.3 0.6 collective-permute-start.19
  114.1 0.5 collective-permute-start.10
  114.6 4.5 %collective-permute-done.19 = f32[96,512]{1,0:T(8,128)S(1)} collective-permute-done((f32[96,512]{1,0:T(8,128)S(1)}, f32[96,512]{1,0:T(8,128)S(1)}, u32[]{:S(2)}, u32[]{:S(2)}) %collective-permute-start.19) | collective-permute-done | bytes 196640 | tf_op jit(solution)/shard_map/ppermute | solution.py:227
  119.1 0.6 gather_fusion.2
  119.7 0.9 fusion
  120.6 4.5 %all-to-all-start.1 = ((f32[16,1,16,512]{3,2,1,0:T(8,128)}), f32[16,1,16,512]{3,2,1,0:T(8,128)S(1)}, u32[]{:S(2)}, u32[]{:S(2)}) async-start(f32[16,1,16,512]{3,2,1,0:T(8,128)} %fusion), calls=%async_computation.1 | async-start | bytes 1048576 | tf_op jit(solution)/shard_map/all_to_all | solution.py:280
  125.1 1.1 constant_dynamic-update-slice_fusion
  126.1 1.0 constant_dynamic-update-slice_fusion.1
  127.2 12.2 %all-to-all-done.1 = f32[16,1,16,512]{3,2,1,0:T(8,128)S(1)} async-done(((f32[16,1,16,512]{3,2,1,0:T(8,128)}), f32[16,1,16,512]{3,2,1,0:T(8,128)S(1)}, u32[]{:S(2)}, u32[]{:S(2)}) %all-to-all-start.1) | async-done | bytes 524320 | tf_op jit(solution)/shard_map/all_to_all | solution.py:280
  139.6 0.7 copy.26
  140.6 0.7 copy.27
  (70 shorter events, 2.7 us)
Async XLA Ops:
  0.6 12.3 %copy-start = (s32[16]{0:T(128)S(1)}, s32[16]{0:T(128)}, u32[]{:S(2)}) copy-start(s32[16]{0:T(128)} %param.13) | copy-start | bytes 196
  0.6 2.0 %copy-start.2 = (f32[128,512]{1,0:T(8,128)S(1)}, f32[128,512]{1,0:T(8,128)}, u32[]{:S(2)}) copy-start(f32[128,512]{1,0:T(8,128)} %param.8) | copy-start | bytes 786436
  0.7 2.1 %copy-start.3 = (f32[128,512]{1,0:T(8,128)S(1)}, f32[128,512]{1,0:T(8,128)}, u32[]{:S(2)}) copy-start(f32[128,512]{1,0:T(8,128)} %param.9) | copy-start | bytes 786436
  2.0 46.3 %collective-permute-start = (f32[128,2048]{1,0:T(8,128)S(1)}, f32[128,2048]{1,0:T(8,128)}, u32[]{:S(2)}, u32[]{:S(2)}) collective-permute-start(f32[128,2048]{1,0:T(8,128)S(1)} %constant_dynamic-slice_fusion.1), channel_id=1, source_target_pairs={{0,1},{1,0},{4,5},{5,4},{8,9},{9,8},{12,13},{13,12},{14,15},{15,14... | collective-permute-start | bytes 3145736 | tf_op jit(solution)/shard_map/ppermute | solution.py:227
  3.2 9.7 %copy-start.13 = (s32[1,6]{1,0:T(1,128)S(1)}, s32[1,6]{1,0:T(1,128)}, u32[]{:S(2)}) copy-start(s32[1,6]{1,0:T(1,128)} %param.12) | copy-start | bytes 76
  4.1 21.3 %all-to-all-start = ((f32[1,16,16,512]{3,2,0,1:T(8,128)}), f32[1,16,16,512]{3,2,0,1:T(8,128)S(1)}, u32[]{:S(2)}, u32[]{:S(2)}) async-start(f32[1,16,16,512]{3,2,0,1:T(8,128)} %bitcast.7), calls=%async_computation | async-start | bytes 1048576 | tf_op jit(solution)/shard_map/all_to_all | solution.py:242
  11.2 36.6 %copy-start.14 = (f32[32]{0:T(128)S(1)}, f32[32]{0:T(128)}, u32[]{:S(2)}) copy-start(f32[32]{0:T(128)} %param.11) | copy-start | bytes 388
  12.5 35.9 %collective-permute-start.1 = (f32[128,2048]{1,0:T(8,128)S(1)}, f32[128,2048]{1,0:T(8,128)}, u32[]{:S(2)}, u32[]{:S(2)}) collective-permute-start(f32[128,2048]{1,0:T(8,128)S(1)} %constant_dynamic-slice_fusion), channel_id=1, source_target_pairs={{0,1},{1,0},{4,5},{5,4},{8,9},{9,8},{12,13},{13,12},{14,15},{15,14... | collective-permute-start | bytes 3145736 | tf_op jit(solution)/shard_map/ppermute | solution.py:227
  26.1 26.1 %copy-start.4 = (f32[96,512]{1,0:T(8,128)}, f32[96,512]{1,0:T(8,128)S(1)}, u32[]{:S(2)}) copy-start(f32[96,512]{1,0:T(8,128)S(1)} %bitcast_select_fusion.1.rest_0_) | copy-start | bytes 589828
  26.1 7.0 %collective-permute-start.2 = (f32[96,512]{1,0:T(8,128)S(1)}, f32[96,512]{1,0:T(8,128)S(1)}, u32[]{:S(2)}, u32[]{:S(2)}) collective-permute-start(f32[96,512]{1,0:T(8,128)S(1)} %bitcast_select_fusion.1.rest_0_), channel_id=1, source_target_pairs={{0,4},{1,5},{4,8},{5,9},{8,12},{9,13},{12,14},{13,15},{14,10},{15,... | collective-permute-start | bytes 589832 | tf_op jit(solution)/shard_map/ppermute | solution.py:227
  27.3 7.6 %collective-permute-start.6 = (f32[96,512]{1,0:T(8,128)S(1)}, f32[96,512]{1,0:T(8,128)S(1)}, u32[]{:S(2)}, u32[]{:S(2)}) collective-permute-start(f32[96,512]{1,0:T(8,128)S(1)} %bitcast_select_fusion.1.rest_0_), channel_id=1, source_target_pairs={{4,0},{5,1},{8,4},{9,5},{12,8},{13,9},{14,12},{15,13},{10,14},{11,... | collective-permute-start | bytes 589832 | tf_op jit(solution)/shard_map/ppermute | solution.py:227
  33.1 19.1 %copy-start.7 = (f32[96,512]{1,0:T(8,128)}, f32[96,512]{1,0:T(8,128)S(1)}, u32[]{:S(2)}) copy-start(f32[96,512]{1,0:T(8,128)S(1)} %collective-permute-done.2.rest_1_) | copy-start | bytes 589828
  33.1 6.4 %collective-permute-start.3 = (f32[96,512]{1,0:T(8,128)S(1)}, f32[96,512]{1,0:T(8,128)S(1)}, u32[]{:S(2)}, u32[]{:S(2)}) collective-permute-start(f32[96,512]{1,0:T(8,128)S(1)} %collective-permute-done.2.rest_1_), channel_id=1, source_target_pairs={{0,4},{1,5},{4,8},{5,9},{8,12},{9,13},{12,14},{13,15},{14,10},{15,... | collective-permute-start | bytes 589832 | tf_op jit(solution)/shard_map/ppermute | solution.py:227
  34.9 17.3 %copy-start.8 = (f32[96,512]{1,0:T(8,128)}, f32[96,512]{1,0:T(8,128)S(1)}, u32[]{:S(2)}) copy-start(f32[96,512]{1,0:T(8,128)S(1)} %collective-permute-done.6.rest_5_) | copy-start | bytes 589828
  34.9 6.7 %collective-permute-start.7 = (f32[96,512]{1,0:T(8,128)S(1)}, f32[96,512]{1,0:T(8,128)S(1)}, u32[]{:S(2)}, u32[]{:S(2)}) collective-permute-start(f32[96,512]{1,0:T(8,128)S(1)} %collective-permute-done.6.rest_5_), channel_id=1, source_target_pairs={{4,0},{5,1},{8,4},{9,5},{12,8},{13,9},{14,12},{15,13},{10,14},{11,... | collective-permute-start | bytes 589832 | tf_op jit(solution)/shard_map/ppermute | solution.py:227
  39.5 12.6 %copy-start.9 = (f32[96,512]{1,0:T(8,128)}, f32[96,512]{1,0:T(8,128)S(1)}, u32[]{:S(2)}) copy-start(f32[96,512]{1,0:T(8,128)S(1)} %collective-permute-done.3.rest_2_) | copy-start | bytes 589828
  39.5 6.1 %collective-permute-start.4 = (f32[96,512]{1,0:T(8,128)S(1)}, f32[96,512]{1,0:T(8,128)S(1)}, u32[]{:S(2)}, u32[]{:S(2)}) collective-permute-start(f32[96,512]{1,0:T(8,128)S(1)} %collective-permute-done.3.rest_2_), channel_id=1, source_target_pairs={{0,4},{1,5},{4,8},{5,9},{8,12},{9,13},{12,14},{13,15},{14,10},{15,... | collective-permute-start | bytes 589832 | tf_op jit(solution)/shard_map/ppermute | solution.py:227
  41.6 10.6 %copy-start.10 = (f32[96,512]{1,0:T(8,128)}, f32[96,512]{1,0:T(8,128)S(1)}, u32[]{:S(2)}) copy-start(f32[96,512]{1,0:T(8,128)S(1)} %collective-permute-done.7.rest_6_) | copy-start | bytes 589828
  41.6 5.9 %collective-permute-start.8 = (f32[96,512]{1,0:T(8,128)S(1)}, f32[96,512]{1,0:T(8,128)S(1)}, u32[]{:S(2)}, u32[]{:S(2)}) collective-permute-start(f32[96,512]{1,0:T(8,128)S(1)} %collective-permute-done.7.rest_6_), channel_id=1, source_target_pairs={{4,0},{5,1},{8,4},{9,5},{12,8},{13,9},{14,12},{15,13},{10,14},{11,... | collective-permute-start | bytes 589832 | tf_op jit(solution)/shard_map/ppermute | solution.py:227
  45.6 6.6 %copy-start.5 = (f32[96,512]{1,0:T(8,128)}, f32[96,512]{1,0:T(8,128)S(1)}, u32[]{:S(2)}) copy-start(f32[96,512]{1,0:T(8,128)S(1)} %collective-permute-done.4.rest_3_) | copy-start | bytes 589828
  45.6 4.7 %collective-permute-start.5 = (f32[48,512]{1,0:T(8,128)S(1)}, f32[48,512]{1,0:T(8,128)S(1)}, u32[]{:S(2)}, u32[]{:S(2)}) collective-permute-start(f32[48,512]{1,0:T(8,128)S(1)} %slice.72), channel_id=1, source_target_pairs={{0,4},{1,5},{4,8},{5,9},{8,12},{9,13},{12,14},{13,15},{14,10},{15,... | collective-permute-start | bytes 294920 | tf_op jit(solution)/shard_map/ppermute | solution.py:227
  47.5 4.7 %copy-start.6 = (f32[96,512]{1,0:T(8,128)}, f32[96,512]{1,0:T(8,128)S(1)}, u32[]{:S(2)}) copy-start(f32[96,512]{1,0:T(8,128)S(1)} %collective-permute-done.8.rest_7_) | copy-start | bytes 589828
  47.5 4.7 %collective-permute-start.9 = (f32[48,512]{1,0:T(8,128)S(1)}, f32[48,512]{1,0:T(8,128)S(1)}, u32[]{:S(2)}, u32[]{:S(2)}) collective-permute-start(f32[48,512]{1,0:T(8,128)S(1)} %slice.73), channel_id=1, source_target_pairs={{4,0},{5,1},{8,4},{9,5},{12,8},{13,9},{14,12},{15,13},{10,14},{11,... | collective-permute-start | bytes 294920 | tf_op jit(solution)/shard_map/ppermute | solution.py:227
  50.3 1.9 %copy-start.11 = (f32[48,512]{1,0:T(8,128)}, f32[48,512]{1,0:T(8,128)S(1)}, u32[]{:S(2)}) copy-start(f32[48,512]{1,0:T(8,128)S(1)} %collective-permute-done.5.rest_4_) | copy-start | bytes 294916
  52.1 0.6 copy-start.12
  86.9 14.5 %copy-start.1 = (f32[768,512]{1,0:T(8,128)S(1)}, f32[768,512]{1,0:T(8,128)}, u32[]{:S(2)}) copy-start(f32[768,512]{1,0:T(8,128)} %get-tuple-element.15) | copy-start | bytes 4718596
  87.9 5.2 %collective-permute-start.12 = (f32[48,512]{1,0:T(8,128)S(1)}, f32[48,512]{1,0:T(8,128)S(1)}, u32[]{:S(2)}, u32[]{:S(2)}) collective-permute-start(f32[48,512]{1,0:T(8,128)S(1)} %slice.57), channel_id=1, source_target_pairs={{4,0},{5,1},{8,4},{9,5},{12,8},{13,9},{14,12},{15,13},{10,14},{11,... | collective-permute-start | bytes 294920 | tf_op jit(solution)/shard_map/ppermute | solution.py:227
  94.1 5.6 %collective-permute-start.16 = (f32[48,512]{1,0:T(8,128)S(1)}, f32[48,512]{1,0:T(8,128)S(1)}, u32[]{:S(2)}, u32[]{:S(2)}) collective-permute-start(f32[48,512]{1,0:T(8,128)S(1)} %get-tuple-element.19), channel_id=1, source_target_pairs={{0,4},{1,5},{4,8},{5,9},{8,12},{9,13},{12,14},{13,15},{14,10},{15,... | collective-permute-start | bytes 294920 | tf_op jit(solution)/shard_map/ppermute | solution.py:227
  94.5 6.8 %collective-permute-start.13 = (f32[96,512]{1,0:T(8,128)S(1)}, f32[96,512]{1,0:T(8,128)S(1)}, u32[]{:S(2)}, u32[]{:S(2)}) collective-permute-start(f32[96,512]{1,0:T(8,128)S(1)} %pad_maximum_fusion.1), channel_id=1, source_target_pairs={{4,0},{5,1},{8,4},{9,5},{12,8},{13,9},{14,12},{15,13},{10,14},{11,... | collective-permute-start | bytes 589832 | tf_op jit(solution)/shard_map/ppermute | solution.py:227
  100.7 6.7 %collective-permute-start.17 = (f32[96,512]{1,0:T(8,128)S(1)}, f32[96,512]{1,0:T(8,128)S(1)}, u32[]{:S(2)}, u32[]{:S(2)}) collective-permute-start(f32[96,512]{1,0:T(8,128)S(1)} %pad_maximum_fusion.2), channel_id=1, source_target_pairs={{0,4},{1,5},{4,8},{5,9},{8,12},{9,13},{12,14},{13,15},{14,10},{15,... | collective-permute-start | bytes 589832 | tf_op jit(solution)/shard_map/ppermute | solution.py:227
  101.4 6.1 %collective-permute-start.14 = (f32[96,512]{1,0:T(8,128)S(1)}, f32[96,512]{1,0:T(8,128)S(1)}, u32[]{:S(2)}, u32[]{:S(2)}) collective-permute-start(f32[96,512]{1,0:T(8,128)S(1)} %slice_add_fusion.2), channel_id=1, source_target_pairs={{4,0},{5,1},{8,4},{9,5},{12,8},{13,9},{14,12},{15,13},{10,14},{11,... | collective-permute-start | bytes 589832 | tf_op jit(solution)/shard_map/ppermute | solution.py:227
  107.5 5.7 %collective-permute-start.18 = (f32[96,512]{1,0:T(8,128)S(1)}, f32[96,512]{1,0:T(8,128)S(1)}, u32[]{:S(2)}, u32[]{:S(2)}) collective-permute-start(f32[96,512]{1,0:T(8,128)S(1)} %get-tuple-element.17), channel_id=1, source_target_pairs={{0,4},{1,5},{4,8},{5,9},{8,12},{9,13},{12,14},{13,15},{14,10},{15,... | collective-permute-start | bytes 589832 | tf_op jit(solution)/shard_map/ppermute | solution.py:227
  108.2 6.4 %collective-permute-start.15 = (f32[96,512]{1,0:T(8,128)S(1)}, f32[96,512]{1,0:T(8,128)S(1)}, u32[]{:S(2)}, u32[]{:S(2)}) collective-permute-start(f32[96,512]{1,0:T(8,128)S(1)} %get-tuple-element.16), channel_id=1, source_target_pairs={{4,0},{5,1},{8,4},{9,5},{12,8},{13,9},{14,12},{15,13},{10,14},{11,... | collective-permute-start | bytes 589832 | tf_op jit(solution)/shard_map/ppermute | solution.py:227
  113.3 5.7 %collective-permute-start.19 = (f32[96,512]{1,0:T(8,128)S(1)}, f32[96,512]{1,0:T(8,128)S(1)}, u32[]{:S(2)}, u32[]{:S(2)}) collective-permute-start(f32[96,512]{1,0:T(8,128)S(1)} %slice_add_fusion.1), channel_id=1, source_target_pairs={{0,4},{1,5},{4,8},{5,9},{8,12},{9,13},{12,14},{13,15},{14,10},{15,... | collective-permute-start | bytes 589832 | tf_op jit(solution)/shard_map/ppermute | solution.py:227
  114.0 11.1 %collective-permute-start.11 = (f32[128,2048]{1,0:T(8,128)}, f32[128,2048]{1,0:T(8,128)S(1)}, u32[]{:S(2)}, u32[]{:S(2)}) collective-permute-start(f32[128,2048]{1,0:T(8,128)} %get-tuple-element.13), channel_id=1, source_target_pairs={{0,1},{1,0},{4,5},{5,4},{8,9},{9,8},{12,13},{13,12},{14,15},{15,14... | collective-permute-start | bytes 3145736 | tf_op jit(solution)/shard_map/ppermute | solution.py:227
  114.1 12.1 %collective-permute-start.10 = (f32[128,2048]{1,0:T(8,128)}, f32[128,2048]{1,0:T(8,128)S(1)}, u32[]{:S(2)}, u32[]{:S(2)}) collective-permute-start(f32[128,2048]{1,0:T(8,128)} %get-tuple-element.11), channel_id=1, source_target_pairs={{0,1},{1,0},{4,5},{5,4},{8,9},{9,8},{12,13},{13,12},{14,15},{15,14... | collective-permute-start | bytes 3145736 | tf_op jit(solution)/shard_map/ppermute | solution.py:227
  120.6 18.7 %all-to-all-start.1 = ((f32[16,1,16,512]{3,2,1,0:T(8,128)}), f32[16,1,16,512]{3,2,1,0:T(8,128)S(1)}, u32[]{:S(2)}, u32[]{:S(2)}) async-start(f32[16,1,16,512]{3,2,1,0:T(8,128)} %fusion), calls=%async_computation.1 | async-start | bytes 1048576 | tf_op jit(solution)/shard_map/all_to_all | solution.py:280
where the time goes:
time: 142 us; the launch traced here: 141 us
  waiting for transfers between devices  61.8 us (44%)
  Pallas kernels  34.1 us (24%)
  starting transfers between devices  28.2 us (20%)
  local copies, waits for them, and re-layouts  12.1 us (9%)
  other arithmetic  4.19 us (3%)
    ppermute x20, waiting for transfers between devices, shift(): return lax.ppermute(x, 'seq', table)  38 us
    pallas_call x1, Pallas kernels, attend(): pl.pallas_call(functools.partial(kernel, n_in, groups, steps, keys), out_...  34.1 us
    ppermute x20, starting transfers between devices, shift(): return lax.ppermute(x, 'seq', table)  16.7 us
    all_to_all x1, waiting for transfers between devices, local(): lax.all_to_all(sent.reshape(devices, blocks_here, piece, width), 'seq', s...  12.2 us
    all_to_all x1, waiting for transfers between devices, local(): x = lax.all_to_all(x, 'seq', split_axis=1, concat_axis=0, tiled=True)  11.6 us
    all_to_all x1, starting transfers between devices, local(): x = lax.all_to_all(x, 'seq', split_axis=1, concat_axis=0, tiled=True)  7.01 us
    all_to_all x1, starting transfers between devices, local(): lax.all_to_all(sent.reshape(devices, blocks_here, piece, width), 'seq', s...  4.45 us
  transfers between devices with their start and end apart: 22, of which 14 were waited for; matrix products, arithmetic and copies ran while one was open for 7% of the time, Pallas kernels for 0%

commit v1 on v0

v1 whole, which is shorter than its diff:
```python
import functools

import jax
import jax.numpy as jnp
from jax import lax
from jax.experimental import pallas as pl
from jax.experimental.pallas import tpu as pltpu
from jax.sharding import PartitionSpec as P


F = 128
BLOCK_TOKENS = 128
WINDOW_ROWS = 2048
CORES = 2
HEADS = 8
CHUNK = 256
VMEM_LIMIT = 32 << 20
LN2 = 0.6931471805599453
LOG2E = 1.4426950408889634
BF = jnp.bfloat16
F32 = jnp.float32


def split(x):
    high = x.astype(BF)
    return high, (x - high.astype(F32)).astype(BF)


def dot(a, b):
    return lax.dot_general(a, b, (((1,), (0,)), ((), ())), preferred_element_type=F32)


def kernel(n_in, groups, steps, keys, gate_ref, q_ref, g_ref, *rest):
    kv_in = rest[:n_in]
    out_ref, dq_ref = rest[n_in : n_in + 2]
    dkv_out = rest[n_in + 2 : 2 * n_in + 2]
    kv, kk, vv, kt, vt, s_ref, d_ref, ph, plo, dh, dlo, dka, dva, sem = rest[2 * n_in + 2 :]
    g, side, p = pl.program_id(0), pl.program_id(1), pl.program_id(2)
    inv_root = F ** (-0.5)
    half = groups * F

    @pl.when((g == 0) & (side == 0) & (p == 0))
    def _():
        copies, at = [], 0
        for i, src in enumerate(kv_in):
            rows = src.shape[0]
            copies.append(pltpu.make_async_copy(src, kv.at[pl.ds(at, rows)], sem.at[i]))
            at += rows
        for c in copies:
            c.start()
        for c in copies:
            c.wait()

    @pl.when((side == 0) & (p == 0))
    def _():
        for off, pack, tr in ((0, kk, kt), (half, vv, vt)):
            x = kv[:, pl.ds(pl.multiple_of(off + g * F, F), F)]
            high, low = split(x)
            pack[:, 0:F] = high
            pack[:, F : 2 * F] = low
            pack[:, 2 * F : 3 * F] = high
            pack[:, 3 * F : 4 * F] = low
            high, low = split(x.T)
            tr[0:F, :] = high
            tr[F : 2 * F, :] = low
        dka[...] = jnp.zeros_like(dka)
        dva[...] = jnp.zeros_like(dva)

    def pack_rows(ref, scale):
        xs = [ref[:, h * F : (h + 1) * F] * scale(h) for h in range(HEADS)]
        rh, rl = split(jnp.concatenate(xs, axis=0))
        cols = jnp.concatenate([y.T for y in xs], axis=1)
        ch, cl = split(cols)
        return jnp.concatenate([rh, rl], axis=1), jnp.concatenate([ch, ch, cl, cl], axis=0), cols

    base = (g * steps + p) * HEADS
    gates = [gate_ref[base + h] for h in range(HEADS)]
    qr, qc, _ = pack_rows(q_ref, lambda h: inv_root * LOG2E)
    ar, ac, acols = pack_rows(g_ref, lambda h: gates[h])

    tiles = [slice(c, c + CHUNK) for c in range(0, keys, CHUNK)]
    m = None
    for t in tiles:
        s = dot(kk[t, :], qc)
        s_ref[t, :] = s
        mc = jnp.max(s, axis=0, keepdims=True)
        m = mc if m is None else jnp.maximum(m, mc)
    l = None
    for t in tiles:
        d_ref[t, :] = dot(vv[t, :], ac)
        e = jnp.exp2(s_ref[t, :] - m)
        s_ref[t, :] = e
        lc = jnp.sum(e, axis=0, keepdims=True)
        l = lc if l is None else l + lc
    inv = 1.0 / l
    for t in tiles:
        w = s_ref[t, :] * inv
        s_ref[t, :] = w
        ph[t, :], plo[t, :] = split(w)
        dva[t, :] += dot(ph[t, :], ar) + dot(plo[t, :], ar)
    o2 = dot(vt[...], ph[...])
    ot = o2[0:F, :] + o2[F : 2 * F, :] + dot(vt[0:F, :], plo[...])
    delta = jnp.sum(ot * acols, axis=0, keepdims=True)
    for t in tiles:
        ds = s_ref[t, :] * (d_ref[t, :] - delta)
        dh[t, :], dlo[t, :] = split(ds)
        dka[t, :] += dot(dh[t, :], qr) + dot(dlo[t, :], qr)
    for h in range(HEADS):
        out_ref[:, h * F : (h + 1) * F] = ot[:, h * F : (h + 1) * F].T * gates[h]
    d2 = dot(kt[...], dh[...])
    dt = (d2[0:F, :] + d2[F : 2 * F, :] + dot(kt[0:F, :], dlo[...])) * inv_root
    for h in range(HEADS):
        dq_ref[:, h * F : (h + 1) * F] = dt[:, h * F : (h + 1) * F].T

    @pl.when((side == pl.num_programs(1) - 1) & (p == steps - 1))
    def _():
        col = pl.multiple_of(g * F, F)
        dk = (dka[:, 0:F] + dka[:, F : 2 * F]) * LN2
        dv = dva[:, 0:F] + dva[:, F : 2 * F]
        at = 0
        for ref in dkv_out:
            rows = ref.shape[0]
            ref[:, pl.ds(col, F)] = dk[at : at + rows]
            ref[:, pl.ds(pl.multiple_of(half + col, F), F)] = dv[at : at + rows]
            at += rows


def attend(gate, q, go, kv_in):
    sides = CORES
    rows = q.shape[0] // sides
    width = kv_in[0].shape[1]
    groups = width // F // 2
    steps = q.shape[1] // F // groups // HEADS
    n_in = len(kv_in)
    keys = sum(x.shape[0] for x in kv_in)
    n = HEADS * rows
    block = pl.BlockSpec((rows, HEADS * F), lambda g, side, p: (side, g * steps + p))
    like = jax.ShapeDtypeStruct(q.shape, F32)
    return pl.pallas_call(
        functools.partial(kernel, n_in, groups, steps, keys),
        out_shape=[like, like] + [jax.ShapeDtypeStruct(x.shape, F32) for x in kv_in],
        grid=(groups, sides, steps),
        in_specs=[pl.BlockSpec(memory_space=pltpu.SMEM), block, block]
        + [pl.BlockSpec(memory_space=pl.ANY)] * n_in,
        out_specs=[block, block] + [pl.BlockSpec(x.shape, lambda g, side, p: (0, 0)) for x in kv_in],
        scratch_shapes=[
            pltpu.VMEM((keys, width), F32),
            pltpu.VMEM((keys, 4 * F), BF),
            pltpu.VMEM((keys, 4 * F), BF),
            pltpu.VMEM((2 * F, keys), BF),
            pltpu.VMEM((2 * F, keys), BF),
            pltpu.VMEM((keys, n), F32),
            pltpu.VMEM((keys, n), F32),
            pltpu.VMEM((keys, n), BF),
            pltpu.VMEM((keys, n), BF),
            pltpu.VMEM((keys, n), BF),
            pltpu.VMEM((keys, n), BF),
            pltpu.VMEM((keys, 2 * F), F32),
            pltpu.VMEM((keys, 2 * F), F32),
            pltpu.SemaphoreType.DMA((n_in,)),
        ],
        compiler_params=pltpu.CompilerParams(
            dimension_semantics=("arbitrary",) * 3, vmem_limit_bytes=VMEM_LIMIT
        ),
        cost_estimate=pl.CostEstimate(
            flops=24 * q.size * keys,
            bytes_accessed=16 * q.size,
            transcendentals=q.size // F * keys,
        ),
        name="attend",
    )(gate, q, go, *kv_in)


def ring_tables(devices, members):
    chips = members // CORES
    order = list(range(0, chips, 2)) + [c for c in range(chips - 1, 0, -1) if c % 2]
    right, left, pair = [], [], []
    for base in range(0, devices, members):
        for at, c in enumerate(order):
            after = order[(at + 1) % chips]
            for core in range(CORES):
                a, b = base + CORES * c + core, base + CORES * after + core
                right.append((a, b))
                left.append((b, a))
                pair.append((a, base + CORES * c + 1 - core))
    return chips, right, left, pair


def local(queries, visual_keys, visual_value_rows, output_gradient, query_head_gate, window_lists, block_place):
    row_count, q_width = queries.shape
    width = visual_keys.shape[1]
    list_len = window_lists.shape[1]
    devices = lax.axis_size("seq")
    members = WINDOW_ROWS // row_count
    windows = devices // members
    blocks_here = visual_keys.shape[0] // BLOCK_TOKENS
    positions = devices * blocks_here
    chips, right, left, pair = ring_tables(devices, members)
    piece = BLOCK_TOKENS // chips
    half_width, q_half = width // CORES, q_width // CORES
    far = chips // 2
    index = lax.axis_index("seq")
    core = index % CORES

    def shift(x, table):
        return lax.ppermute(x, "seq", table)

    mine = lax.dynamic_index_in_dim(window_lists, index // members, 0, keepdims=False)
    wanted = jnp.take(block_place, mine, axis=0)

    def half(x, which):
        return lax.dynamic_slice_in_dim(x, which * q_half, q_half, 1)

    def both(x):
        mine, theirs = half(x, core), half(x, 1 - core)
        return jnp.concatenate([mine, shift(theirs, pair)], axis=0)

    def for_core(c):
        cols = slice(c * half_width, (c + 1) * half_width)
        x = jnp.concatenate([visual_keys[:, cols], visual_value_rows[:, cols]], axis=1)
        return x.reshape(blocks_here, chips, 1, piece, width)

    x = jnp.concatenate([for_core(c) for c in range(CORES)], axis=2).reshape(blocks_here, members, piece, width)
    x = jnp.tile(x, (1, windows, 1, 1))
    x, queries, output_gradient = lax.optimization_barrier((x, queries, output_gradient))
    x = lax.all_to_all(x, "seq", split_axis=1, concat_axis=0, tiled=True)
    q_both, g_both = both(queries), both(output_gradient)
    x = jnp.take(x.reshape(positions, piece, width), wanted, axis=0).reshape(list_len * piece, width)

    n = x.shape[0]
    cut = n // 2
    rights, lefts = [], []
    r = l = x
    for step in range(1, far + 1):
        if step == far:
            r, l = r[:cut], l[cut:]
        r, l = shift(r, right), shift(l, left)
        rights.append(r)
        lefts.append(l)
    chunks = [x] + rights + lefts
    gate = lax.dynamic_slice_in_dim(jnp.tanh(query_head_gate), core * (q_half // F), q_half // F, 0)
    out, dq, *parts = attend(gate, q_both, g_both, chunks)
    rights, lefts = parts[1 : 1 + far], parts[1 + far :]
    r, l = shift(rights[-1], left), shift(lefts[-1], right)
    for step in range(far - 1, 0, -1):
        r, l = lax.optimization_barrier((r, l))
        a, b = rights[step - 1], lefts[step - 1]
        if step == far - 1:
            a = jnp.concatenate([a[:cut] + r, a[cut:]], axis=0)
            b = jnp.concatenate([b[:cut], b[cut:] + l], axis=0)
        else:
            a, b = a + r, b + l
        a, b = lax.optimization_barrier((a, b))
        r, l = shift(a, left), shift(b, right)
    out_back, dq_back = shift(out[row_count:], pair), shift(dq[row_count:], pair)
    total = (parts[0] + r + l).reshape(list_len, piece, width)
    hit = wanted[None, :] == jnp.arange(positions, dtype=jnp.int32)[:, None]
    slot = jnp.argmax(hit, axis=1)
    sent = jnp.where(jnp.any(hit, axis=1)[:, None, None], jnp.take(total, slot, axis=0), 0.0)
    back = lax.all_to_all(
        sent.reshape(devices, blocks_here, piece, width), "seq", split_axis=0, concat_axis=0, tiled=True
    ).reshape(windows, chips, CORES, blocks_here, piece, width)
    back = back[0] if windows == 1 else jnp.sum(back, axis=0)

    def by_rows(x):
        return x.transpose(2, 0, 3, 1, 4).reshape(blocks_here * BLOCK_TOKENS, width)

    def whole(x, y):
        x = x[:row_count]
        return jnp.where(core == 0, jnp.concatenate([x, y], axis=1), jnp.concatenate([y, x], axis=1))

    return (
        whole(out, out_back),
        whole(dq, dq_back),
        by_rows(back[..., :half_width]),
        by_rows(back[..., half_width:]),
    )


def solution(mesh):
    rows = P(("parts", "seq"), None)
    return jax.shard_map(
        local,
        mesh=mesh,
        in_specs=(rows, rows, rows, rows, P(), P("parts", None), P("parts")),
        out_specs=(rows, rows, rows, rows),
        check_vma=False,
    )
```

time: 142 us -> 133 us (0.937)
  waiting for transfers between devices: 61.8 us -> 51.8 us
  other arithmetic: 4.19 us -> 12.4 us
  Pallas kernels: 34.1 us -> 26.4 us
    pallas_call x1, Pallas kernels: 34.1 us -> 26.4 us  [attend(): pl.pallas_call(functools.partial(kernel, n_in, groups, steps, keys), out_...]
    ppermute x20, waiting for transfers between devices: 38 us -> 30.7 us  [shift(): return lax.ppermute(x, 'seq', table)]
    select_n x0 -> x2, other arithmetic: none -> 6.47 us  [whole(): jnp.where(core == 0, jnp.concatenate([x, y], axis=1), jnp.concatenate([y,...]
    all_to_all x1, waiting for transfers between devices: 12.2 us -> 7.79 us  [local(): lax.all_to_all(sent.reshape(devices, blocks_here, piece, width), 'seq', s...]
    concatenate x1 -> x4, other arithmetic: 0.27 us -> 3.99 us  [the longest x2 3.09 us: both(): return jnp.concatenate([mine, shift(theirs, pair)], axis=0)]
    slice x1 -> x4, local copies, waits for them, and re-layouts: 1.02 us -> 4.29 us  [the longest x2 2.32 us: whole(): x = x[:row_count]]
    dynamic_update_slice x2 -> x0, local copies, waits for them, and re-layouts: 2.1 us -> none  [whole(): return lax.dynamic_update_slice_in_dim(x, y, (1 - core) * q_half, 1)]
    all_to_all x1, waiting for transfers between devices: 11.6 us -> 13.3 us  [local(): x = lax.all_to_all(x, 'seq', split_axis=1, concat_axis=0, tiled=True)]
  transfers between devices with their start and end apart: 22 -> 22, of which waited for: 14 -> 14; matrix products, arithmetic and copies ran while one was open for 7% -> 13% of each run, Pallas kernels for 0% -> 0%
where the time goes in v1:
time: 133 us
  waiting for transfers between devices  51.8 us (39%)
  starting transfers between devices  28.9 us (22%)
  Pallas kernels  26.4 us (20%)
  other arithmetic  12.4 us (9%)
  local copies, waits for them, and re-layouts  12.3 us (9%)
    ppermute x20, waiting for transfers between devices, shift(): return lax.ppermute(x, 'seq', table)  30.7 us
    pallas_call x1, Pallas kernels, attend(): pl.pallas_call(functools.partial(kernel, n_in, groups, steps, keys), out_...  26.4 us
    ppermute x20, starting transfers between devices, shift(): return lax.ppermute(x, 'seq', table)  17.2 us
    all_to_all x1, waiting for transfers between devices, local(): x = lax.all_to_all(x, 'seq', split_axis=1, concat_axis=0, tiled=True)  13.3 us
    all_to_all x1, waiting for transfers between devices, local(): lax.all_to_all(sent.reshape(devices, blocks_here, piece, width), 'seq', s...  7.79 us
    all_to_all x1, starting transfers between devices, local(): x = lax.all_to_all(x, 'seq', split_axis=1, concat_axis=0, tiled=True)  7.43 us
    select_n x2, other arithmetic, whole(): jnp.where(core == 0, jnp.concatenate([x, y], axis=1), jnp.concatenate([y,...  6.47 us
    all_to_all x1, starting transfers between devices, local(): lax.all_to_all(sent.reshape(devices, blocks_here, piece, width), 'seq', s...  4.21 us
  transfers between devices with their start and end apart: 22, of which 14 were waited for; matrix products, arithmetic and copies ran while one was open for 13% of the time, Pallas kernels for 0%

profile of v1, /device:TPU:0, one launch (start us, length us, event | category | flops | bytes accessed | tf_op | source)
XLA Modules:
  0.0 132.8 jit_solution(17169115933977957606)
XLA Ops:
  0.7 1.0 fusion.7
  1.7 1.0 fusion.8
  2.7 0.8 pad_maximum_fusion.2
  3.6 2.8 %constant_dynamic-slice_fusion.1 = (f32[128,2048]{1,0:T(8,128)S(1)}, f32[128,2048]{1,0:T(8,128)}) fusion(f32[128,4096]{1,0:T(8,128)} %param.10, s32[]{:T(128)S(6)} %select_n.131, s32[]{:T(128)S(6)} %select_n.132), kind=kLoop, calls=%fused_computation.38 | loop fusion | bytes 4194312 | tf_op jit(solution)/shard_map/dynamic_slice | solution.py:212
  6.4 0.5 collective-permute-start.1
  7.2 7.4 %all-to-all-start = ((f32[1,16,16,512]{3,2,0,1:T(8,128)}), f32[1,16,16,512]{3,2,0,1:T(8,128)}, u32[]{:S(2)}, u32[]{:S(2)}) async-start(f32[1,16,16,512]{3,2,0,1:T(8,128)} %bitcast.6), calls=%async_computation | async-start | bytes 1048576 | tf_op jit(solution)/shard_map/all_to_all | solution.py:226
  14.7 0.6 gather_fusion
  15.6 13.3 %all-to-all-done = f32[1,16,16,512]{3,2,0,1:T(8,128)} async-done(((f32[1,16,16,512]{3,2,0,1:T(8,128)}), f32[1,16,16,512]{3,2,0,1:T(8,128)}, u32[]{:S(2)}, u32[]{:S(2)}) %all-to-all-start) | async-done | bytes 524320 | tf_op jit(solution)/shard_map/all_to_all | solution.py:226
  28.9 1.6 %gather_fusion.1 = f32[6,16,512]{2,1,0:T(8,128)S(1)} fusion(f32[16,16,512]{2,1,0:T(8,128)} %bitcast.7, s32[1024]{0:T(1024)S(1)} %pad_clamp_fusion.1), kind=kCustom, calls=%fused_computation.1 | custom fusion | bytes 393240 | tf_op jit(solution)/shard_map/jit(_take)/gather | solution.py:228
  30.6 1.2 collective-permute-start.2
  31.8 0.9 collective-permute-start.6
  32.7 0.6 iota_reduce_fusion
  33.3 4.3 %collective-permute-done.2.rest_1_ = f32[96,512]{1,0:T(8,128)S(1)} collective-permute-done((f32[96,512]{1,0:T(8,128)S(1)}, f32[96,512]{1,0:T(8,128)S(1)}, u32[]{:S(2)}, u32[]{:S(2)}) %collective-permute-start.2) | collective-permute-done | bytes 196640 | tf_op jit(solution)/shard_map/ppermute | solution.py:206
  37.6 1.7 %collective-permute-start.3 = (f32[96,512]{1,0:T(8,128)S(1)}, f32[96,512]{1,0:T(8,128)S(1)}, u32[]{:S(2)}, u32[]{:S(2)}) collective-permute-start(f32[96,512]{1,0:T(8,128)S(1)} %collective-permute-done.2.rest_1_), channel_id=1, source_target_pairs={{0,4},{1,5},{4,8},{5,9},{8,12},{9,13},{12,14},{13,15},{14,10},{15,... | collective-permute-start | bytes 589832 | tf_op jit(solution)/shard_map/ppermute | solution.py:206
  39.7 4.4 %collective-permute-done.3.rest_2_ = f32[96,512]{1,0:T(8,128)S(1)} collective-permute-done((f32[96,512]{1,0:T(8,128)S(1)}, f32[96,512]{1,0:T(8,128)S(1)}, u32[]{:S(2)}, u32[]{:S(2)}) %collective-permute-start.3) | collective-permute-done | bytes 196640 | tf_op jit(solution)/shard_map/ppermute | solution.py:206
  44.1 2.0 %collective-permute-start.4 = (f32[96,512]{1,0:T(8,128)S(1)}, f32[96,512]{1,0:T(8,128)S(1)}, u32[]{:S(2)}, u32[]{:S(2)}) collective-permute-start(f32[96,512]{1,0:T(8,128)S(1)} %collective-permute-done.3.rest_2_), channel_id=1, source_target_pairs={{0,4},{1,5},{4,8},{5,9},{8,12},{9,13},{12,14},{13,15},{14,10},{15,... | collective-permute-start | bytes 589832 | tf_op jit(solution)/shard_map/ppermute | solution.py:206
  46.1 1.5 %pad_maximum_fusion.1.g_ref = f32[256,2048]{1,0:T(8,128)S(1)} fusion(f32[128,2048]{1,0:T(8,128)} %collective-permute-done.1, f32[128,2048]{1,0:T(8,128)S(1)} %get-tuple-element.62), kind=kLoop, calls=%fused_computation.4 | loop fusion | flops 524288 | bytes 4194304 | tf_op jit(solution)/shard_map/concatenate | solution.py:216
  47.7 2.5 %collective-permute-done.4.rest_3_ = f32[96,512]{1,0:T(8,128)S(1)} collective-permute-done((f32[96,512]{1,0:T(8,128)S(1)}, f32[96,512]{1,0:T(8,128)S(1)}, u32[]{:S(2)}, u32[]{:S(2)}) %collective-permute-start.4) | collective-permute-done | bytes 196640 | tf_op jit(solution)/shard_map/ppermute | solution.py:206
  50.2 1.8 %collective-permute-start.5 = (f32[48,512]{1,0:T(8,128)S(1)}, f32[48,512]{1,0:T(8,128)S(1)}, u32[]{:S(2)}, u32[]{:S(2)}) collective-permute-start(f32[48,512]{1,0:T(8,128)S(1)} %slice.70), channel_id=1, source_target_pairs={{0,4},{1,5},{4,8},{5,9},{8,12},{9,13},{12,14},{13,15},{14,10},{15,... | collective-permute-start | bytes 294920 | tf_op jit(solution)/shard_map/ppermute | solution.py:206
  52.0 0.3 collective-permute-start.9
  52.3 1.5 %pad_maximum_fusion.q_ref = f32[256,2048]{1,0:T(8,128)S(1)} fusion(f32[128,2048]{1,0:T(8,128)} %collective-permute-done, f32[128,2048]{1,0:T(8,128)S(1)} %get-tuple-element.64), kind=kLoop, calls=%fused_computation.3 | loop fusion | flops 524288 | bytes 4194304 | tf_op jit(solution)/shard_map/concatenate | solution.py:216
  53.9 1.0 collective-permute-done.5.rest_4_
  54.8 1.9 %collective-permute-done.9.rest_8_ = f32[48,512]{1,0:T(8,128)S(1)} collective-permute-done((f32[48,512]{1,0:T(8,128)S(1)}, f32[48,512]{1,0:T(8,128)S(1)}, u32[]{:S(2)}, u32[]{:S(2)}) %collective-permute-start.9) | collective-permute-done | bytes 98336 | tf_op jit(solution)/shard_map/ppermute | solution.py:206
  56.7 26.4 %attend.1 = (f32[256,2048]{1,0:T(8,128)S(1)}, f32[256,2048]{1,0:T(8,128)S(1)}, f32[96,512]{1,0:T(8,128)S(1)}, f32[96,512]{1,0:T(8,128)S(1)}, f32[96,512]{1,0:T(8...) custom-call(f32[16]{0:T(128)S(1)} %dynamic_slice.17.gate_ref, ...), custom_call_target="tpu_custom_call" | custom-call | flops 9663676416 | bytes 8388608 | tf_op jit(solution)/shard_map/attend/pallas_call | solution.py:139
  83.1 0.3 collective-permute-start.12
  83.4 1.8 %collective-permute-start.13 = (f32[48,512]{1,0:T(8,128)S(1)}, f32[48,512]{1,0:T(8,128)S(1)}, u32[]{:S(2)}, u32[]{:S(2)}) collective-permute-start(f32[48,512]{1,0:T(8,128)S(1)} %get-tuple-element.42), channel_id=1, source_target_pairs={{0,4},{1,5},{4,8},{5,9},{8,12},{9,13},{12,14},{13,15},{14,10},{15,... | collective-permute-start | bytes 294920 | tf_op jit(solution)/shard_map/ppermute | solution.py:206
  85.2 3.6 %collective-permute-done.12 = f32[48,512]{1,0:T(8,128)S(1)} collective-permute-done((f32[48,512]{1,0:T(8,128)S(1)}, f32[48,512]{1,0:T(8,128)S(1)}, u32[]{:S(2)}, u32[]{:S(2)}) %collective-permute-start.12) | collective-permute-done | bytes 98336 | tf_op jit(solution)/shard_map/ppermute | solution.py:206
  88.9 2.0 %collective-permute-start.14 = (f32[96,512]{1,0:T(8,128)S(1)}, f32[96,512]{1,0:T(8,128)S(1)}, u32[]{:S(2)}, u32[]{:S(2)}) collective-permute-start(f32[96,512]{1,0:T(8,128)S(1)} %pad_maximum_fusion.5), channel_id=1, source_target_pairs={{4,0},{5,1},{8,4},{9,5},{12,8},{13,9},{14,12},{15,13},{10,14},{11,... | collective-permute-start | bytes 589832 | tf_op jit(solution)/shard_map/ppermute | solution.py:206
  91.1 5.6 %collective-permute-done.14 = f32[96,512]{1,0:T(8,128)S(1)} collective-permute-done((f32[96,512]{1,0:T(8,128)S(1)}, f32[96,512]{1,0:T(8,128)S(1)}, u32[]{:S(2)}, u32[]{:S(2)}) %collective-permute-start.14) | collective-permute-done | bytes 196640 | tf_op jit(solution)/shard_map/ppermute | solution.py:206
  96.6 1.1 collective-permute-done.15
  97.8 0.4 collective-permute-start.16
  98.2 1.7 %collective-permute-start.17 = (f32[96,512]{1,0:T(8,128)S(1)}, f32[96,512]{1,0:T(8,128)S(1)}, u32[]{:S(2)}, u32[]{:S(2)}) collective-permute-start(f32[96,512]{1,0:T(8,128)S(1)} %add.98), channel_id=1, source_target_pairs={{0,4},{1,5},{4,8},{5,9},{8,12},{9,13},{12,14},{13,15},{14,10},{15,... | collective-permute-start | bytes 589832 | tf_op jit(solution)/shard_map/ppermute | solution.py:206
  99.9 1.2 fusion.5
  101.0 2.5 %collective-permute-done.16 = f32[96,512]{1,0:T(8,128)S(1)} collective-permute-done((f32[96,512]{1,0:T(8,128)S(1)}, f32[96,512]{1,0:T(8,128)S(1)}, u32[]{:S(2)}, u32[]{:S(2)}) %collective-permute-start.16) | collective-permute-done | bytes 196640 | tf_op jit(solution)/shard_map/ppermute | solution.py:206
  103.5 0.3 collective-permute-done.17
  103.9 1.2 collective-permute-start.18
  105.2 0.9 collective-permute-start.19
  106.0 1.2 fusion.6
  107.2 2.5 %collective-permute-done.18 = f32[96,512]{1,0:T(8,128)S(1)} collective-permute-done((f32[96,512]{1,0:T(8,128)S(1)}, f32[96,512]{1,0:T(8,128)S(1)}, u32[]{:S(2)}, u32[]{:S(2)}) %collective-permute-start.18) | collective-permute-done | bytes 196640 | tf_op jit(solution)/shard_map/ppermute | solution.py:206
  109.6 1.2 collective-permute-done.19
  110.9 0.6 gather_fusion.2
  111.5 0.9 fusion
  112.4 4.2 %all-to-all-start.1 = ((f32[16,1,16,512]{3,2,1,0:T(8,128)}), f32[16,1,16,512]{3,2,1,0:T(8,128)S(1)}, u32[]{:S(2)}, u32[]{:S(2)}) async-start(f32[16,1,16,512]{3,2,1,0:T(8,128)} %fusion), calls=%async_computation.1 | async-start | bytes 1048576 | tf_op jit(solution)/shard_map/all_to_all | solution.py:260
  116.6 3.2 %maximum_select_fusion.1 = f32[128,4096]{1,0:T(8,128)} fusion(f32[128,2048]{1,0:T(8,128)} %collective-permute-done.11, f32[128,2048]{1,0:T(8,128)S(1)} %get-tuple-element.58, pred[]{:T(512)S(6)} %eq.23), kind=kLoop, calls=%fused_computation.6 | loop fusion | flops 1572864 | bytes 4194305 | tf_op jit(solution)/shard_map/jit(_where)/select_n | solution.py:270
  119.8 3.2 %maximum_select_fusion = f32[128,4096]{1,0:T(8,128)} fusion(f32[128,2048]{1,0:T(8,128)} %collective-permute-done.10, f32[128,2048]{1,0:T(8,128)S(1)} %get-tuple-element.60, pred[]{:T(512)S(6)} %eq.23), kind=kLoop, calls=%fused_computation.5 | loop fusion | flops 1572864 | bytes 4194305 | tf_op jit(solution)/shard_map/jit(_where)/select_n | solution.py:270
  123.1 7.8 %all-to-all-done.1 = f32[16,1,16,512]{3,2,1,0:T(8,128)S(1)} async-done(((f32[16,1,16,512]{3,2,1,0:T(8,128)}), f32[16,1,16,512]{3,2,1,0:T(8,128)S(1)}, u32[]{:S(2)}, u32[]{:S(2)}) %all-to-all-start.1) | async-done | bytes 524320 | tf_op jit(solution)/shard_map/all_to_all | solution.py:260
  131.1 0.7 copy.21
  132.1 0.7 copy.22
  (53 shorter events, 1.9 us)
Async XLA Ops:
  0.6 14.0 %copy-start = (s32[16]{0:T(128)S(1)}, s32[16]{0:T(128)}, u32[]{:S(2)}) copy-start(s32[16]{0:T(128)} %param.13) | copy-start | bytes 196
  3.6 3.3 %copy-start.1 = (f32[128,4096]{1,0:T(8,128)S(1)}, f32[128,4096]{1,0:T(8,128)}, u32[]{:S(2)}) copy-start(f32[128,4096]{1,0:T(8,128)} %param.7) | copy-start | bytes 6291460
  6.4 8.2 %copy-start.3 = (s32[1,6]{1,0:T(1,128)S(1)}, s32[1,6]{1,0:T(1,128)}, u32[]{:S(2)}) copy-start(s32[1,6]{1,0:T(1,128)} %param.12) | copy-start | bytes 76
  6.4 8.9 %copy-start.2 = (f32[32]{0:T(128)S(1)}, f32[32]{0:T(128)}, u32[]{:S(2)}) copy-start(f32[32]{0:T(128)} %param.11) | copy-start | bytes 388
  6.4 39.7 %collective-permute-start.1 = (f32[128,2048]{1,0:T(8,128)}, f32[128,2048]{1,0:T(8,128)}, u32[]{:S(2)}, u32[]{:S(2)}) collective-permute-start(f32[128,2048]{1,0:T(8,128)} %get-tuple-element.63), channel_id=1, source_target_pairs={{0,1},{1,0},{4,5},{5,4},{8,9},{9,8},{12,13},{13,12},{14,15},{15,14... | collective-permute-start | bytes 3145736 | tf_op jit(solution)/shard_map/ppermute | solution.py:206
  7.1 45.2 %collective-permute-start = (f32[128,2048]{1,0:T(8,128)S(1)}, f32[128,2048]{1,0:T(8,128)}, u32[]{:S(2)}, u32[]{:S(2)}) collective-permute-start(f32[128,2048]{1,0:T(8,128)S(1)} %get-tuple-element.65), channel_id=1, source_target_pairs={{0,1},{1,0},{4,5},{5,4},{8,9},{9,8},{12,13},{13,12},{14,15},{15,14... | collective-permute-start | bytes 3145736 | tf_op jit(solution)/shard_map/ppermute | solution.py:206
  7.2 21.8 %all-to-all-start = ((f32[1,16,16,512]{3,2,0,1:T(8,128)}), f32[1,16,16,512]{3,2,0,1:T(8,128)}, u32[]{:S(2)}, u32[]{:S(2)}) async-start(f32[1,16,16,512]{3,2,0,1:T(8,128)} %bitcast.6), calls=%async_computation | async-start | bytes 1048576 | tf_op jit(solution)/shard_map/all_to_all | solution.py:226
  30.6 7.0 %collective-permute-start.2 = (f32[96,512]{1,0:T(8,128)S(1)}, f32[96,512]{1,0:T(8,128)S(1)}, u32[]{:S(2)}, u32[]{:S(2)}) collective-permute-start(f32[96,512]{1,0:T(8,128)S(1)} %bitcast_select_fusion.1.rest_0_), channel_id=1, source_target_pairs={{0,4},{1,5},{4,8},{5,9},{8,12},{9,13},{12,14},{13,15},{14,10},{15,... | collective-permute-start | bytes 589832 | tf_op jit(solution)/shard_map/ppermute | solution.py:206
  31.8 7.6 %collective-permute-start.6 = (f32[96,512]{1,0:T(8,128)S(1)}, f32[96,512]{1,0:T(8,128)S(1)}, u32[]{:S(2)}, u32[]{:S(2)}) collective-permute-start(f32[96,512]{1,0:T(8,128)S(1)} %bitcast_select_fusion.1.rest_0_), channel_id=1, source_target_pairs={{4,0},{5,1},{8,4},{9,5},{12,8},{13,9},{14,12},{15,13},{10,14},{11,... | collective-permute-start | bytes 589832 | tf_op jit(solution)/shard_map/ppermute | solution.py:206
  37.6 6.4 %collective-permute-start.3 = (f32[96,512]{1,0:T(8,128)S(1)}, f32[96,512]{1,0:T(8,128)S(1)}, u32[]{:S(2)}, u32[]{:S(2)}) collective-permute-start(f32[96,512]{1,0:T(8,128)S(1)} %collective-permute-done.2.rest_1_), channel_id=1, source_target_pairs={{0,4},{1,5},{4,8},{5,9},{8,12},{9,13},{12,14},{13,15},{14,10},{15,... | collective-permute-start | bytes 589832 | tf_op jit(solution)/shard_map/ppermute | solution.py:206
  39.4 6.7 %collective-permute-start.7 = (f32[96,512]{1,0:T(8,128)S(1)}, f32[96,512]{1,0:T(8,128)S(1)}, u32[]{:S(2)}, u32[]{:S(2)}) collective-permute-start(f32[96,512]{1,0:T(8,128)S(1)} %collective-permute-done.6.rest_5_), channel_id=1, source_target_pairs={{4,0},{5,1},{8,4},{9,5},{12,8},{13,9},{14,12},{15,13},{10,14},{11,... | collective-permute-start | bytes 589832 | tf_op jit(solution)/shard_map/ppermute | solution.py:206
  44.1 6.1 %collective-permute-start.4 = (f32[96,512]{1,0:T(8,128)S(1)}, f32[96,512]{1,0:T(8,128)S(1)}, u32[]{:S(2)}, u32[]{:S(2)}) collective-permute-start(f32[96,512]{1,0:T(8,128)S(1)} %collective-permute-done.3.rest_2_), channel_id=1, source_target_pairs={{0,4},{1,5},{4,8},{5,9},{8,12},{9,13},{12,14},{13,15},{14,10},{15,... | collective-permute-start | bytes 589832 | tf_op jit(solution)/shard_map/ppermute | solution.py:206
  46.1 5.9 %collective-permute-start.8 = (f32[96,512]{1,0:T(8,128)S(1)}, f32[96,512]{1,0:T(8,128)S(1)}, u32[]{:S(2)}, u32[]{:S(2)}) collective-permute-start(f32[96,512]{1,0:T(8,128)S(1)} %collective-permute-done.7.rest_6_), channel_id=1, source_target_pairs={{4,0},{5,1},{8,4},{9,5},{12,8},{13,9},{14,12},{15,13},{10,14},{11,... | collective-permute-start | bytes 589832 | tf_op jit(solution)/shard_map/ppermute | solution.py:206
  50.2 4.7 %collective-permute-start.5 = (f32[48,512]{1,0:T(8,128)S(1)}, f32[48,512]{1,0:T(8,128)S(1)}, u32[]{:S(2)}, u32[]{:S(2)}) collective-permute-start(f32[48,512]{1,0:T(8,128)S(1)} %slice.70), channel_id=1, source_target_pairs={{0,4},{1,5},{4,8},{5,9},{8,12},{9,13},{12,14},{13,15},{14,10},{15,... | collective-permute-start | bytes 294920 | tf_op jit(solution)/shard_map/ppermute | solution.py:206
  52.0 4.7 %collective-permute-start.9 = (f32[48,512]{1,0:T(8,128)S(1)}, f32[48,512]{1,0:T(8,128)S(1)}, u32[]{:S(2)}, u32[]{:S(2)}) collective-permute-start(f32[48,512]{1,0:T(8,128)S(1)} %slice.71), channel_id=1, source_target_pairs={{4,0},{5,1},{8,4},{9,5},{12,8},{13,9},{14,12},{15,13},{10,14},{11,... | collective-permute-start | bytes 294920 | tf_op jit(solution)/shard_map/ppermute | solution.py:206
  83.1 5.7 %collective-permute-start.12 = (f32[48,512]{1,0:T(8,128)S(1)}, f32[48,512]{1,0:T(8,128)S(1)}, u32[]{:S(2)}, u32[]{:S(2)}) collective-permute-start(f32[48,512]{1,0:T(8,128)S(1)} %get-tuple-element.41), channel_id=1, source_target_pairs={{4,0},{5,1},{8,4},{9,5},{12,8},{13,9},{14,12},{15,13},{10,14},{11,... | collective-permute-start | bytes 294920 | tf_op jit(solution)/shard_map/ppermute | solution.py:206
  83.4 5.4 %collective-permute-start.13 = (f32[48,512]{1,0:T(8,128)S(1)}, f32[48,512]{1,0:T(8,128)S(1)}, u32[]{:S(2)}, u32[]{:S(2)}) collective-permute-start(f32[48,512]{1,0:T(8,128)S(1)} %get-tuple-element.42), channel_id=1, source_target_pairs={{0,4},{1,5},{4,8},{5,9},{8,12},{9,13},{12,14},{13,15},{14,10},{15,... | collective-permute-start | bytes 294920 | tf_op jit(solution)/shard_map/ppermute | solution.py:206
  88.9 7.7 %collective-permute-start.14 = (f32[96,512]{1,0:T(8,128)S(1)}, f32[96,512]{1,0:T(8,128)S(1)}, u32[]{:S(2)}, u32[]{:S(2)}) collective-permute-start(f32[96,512]{1,0:T(8,128)S(1)} %pad_maximum_fusion.5), channel_id=1, source_target_pairs={{4,0},{5,1},{8,4},{9,5},{12,8},{13,9},{14,12},{15,13},{10,14},{11,... | collective-permute-start | bytes 589832 | tf_op jit(solution)/shard_map/ppermute | solution.py:206
  90.9 6.8 %collective-permute-start.15 = (f32[96,512]{1,0:T(8,128)S(1)}, f32[96,512]{1,0:T(8,128)S(1)}, u32[]{:S(2)}, u32[]{:S(2)}) collective-permute-start(f32[96,512]{1,0:T(8,128)S(1)} %pad_maximum_fusion.6), channel_id=1, source_target_pairs={{0,4},{1,5},{4,8},{5,9},{8,12},{9,13},{12,14},{13,15},{14,10},{15,... | collective-permute-start | bytes 589832 | tf_op jit(solution)/shard_map/ppermute | solution.py:206
  97.8 5.7 %collective-permute-start.16 = (f32[96,512]{1,0:T(8,128)S(1)}, f32[96,512]{1,0:T(8,128)S(1)}, u32[]{:S(2)}, u32[]{:S(2)}) collective-permute-start(f32[96,512]{1,0:T(8,128)S(1)} %add.97), channel_id=1, source_target_pairs={{4,0},{5,1},{8,4},{9,5},{12,8},{13,9},{14,12},{15,13},{10,14},{11,... | collective-permute-start | bytes 589832 | tf_op jit(solution)/shard_map/ppermute | solution.py:206
  98.2 5.7 %collective-permute-start.17 = (f32[96,512]{1,0:T(8,128)S(1)}, f32[96,512]{1,0:T(8,128)S(1)}, u32[]{:S(2)}, u32[]{:S(2)}) collective-permute-start(f32[96,512]{1,0:T(8,128)S(1)} %add.98), channel_id=1, source_target_pairs={{0,4},{1,5},{4,8},{5,9},{8,12},{9,13},{12,14},{13,15},{14,10},{15,... | collective-permute-start | bytes 589832 | tf_op jit(solution)/shard_map/ppermute | solution.py:206
  101.0 15.6 %collective-permute-start.11 = (f32[128,2048]{1,0:T(8,128)}, f32[128,2048]{1,0:T(8,128)}, u32[]{:S(2)}, u32[]{:S(2)}) collective-permute-start(f32[128,2048]{1,0:T(8,128)} %get-tuple-element.59), channel_id=1, source_target_pairs={{0,1},{1,0},{4,5},{5,4},{8,9},{9,8},{12,13},{13,12},{14,15},{15,14... | collective-permute-start | bytes 3145736 | tf_op jit(solution)/shard_map/ppermute | solution.py:206
  103.9 5.7 %collective-permute-start.18 = (f32[96,512]{1,0:T(8,128)S(1)}, f32[96,512]{1,0:T(8,128)S(1)}, u32[]{:S(2)}, u32[]{:S(2)}) collective-permute-start(f32[96,512]{1,0:T(8,128)S(1)} %add.99), channel_id=1, source_target_pairs={{4,0},{5,1},{8,4},{9,5},{12,8},{13,9},{14,12},{15,13},{10,14},{11,... | collective-permute-start | bytes 589832 | tf_op jit(solution)/shard_map/ppermute | solution.py:206
  105.2 5.7 %collective-permute-start.19 = (f32[96,512]{1,0:T(8,128)S(1)}, f32[96,512]{1,0:T(8,128)S(1)}, u32[]{:S(2)}, u32[]{:S(2)}) collective-permute-start(f32[96,512]{1,0:T(8,128)S(1)} %add.100), channel_id=1, source_target_pairs={{0,4},{1,5},{4,8},{5,9},{8,12},{9,13},{12,14},{13,15},{14,10},{15,... | collective-permute-start | bytes 589832 | tf_op jit(solution)/shard_map/ppermute | solution.py:206
  107.2 12.7 %collective-permute-start.10 = (f32[128,2048]{1,0:T(8,128)}, f32[128,2048]{1,0:T(8,128)}, u32[]{:S(2)}, u32[]{:S(2)}) collective-permute-start(f32[128,2048]{1,0:T(8,128)} %get-tuple-element.61), channel_id=1, source_target_pairs={{0,1},{1,0},{4,5},{5,4},{8,9},{9,8},{12,13},{13,12},{14,15},{15,14... | collective-permute-start | bytes 3145736 | tf_op jit(solution)/shard_map/ppermute | solution.py:206
  112.4 18.5 %all-to-all-start.1 = ((f32[16,1,16,512]{3,2,1,0:T(8,128)}), f32[16,1,16,512]{3,2,1,0:T(8,128)S(1)}, u32[]{:S(2)}, u32[]{:S(2)}) async-start(f32[16,1,16,512]{3,2,1,0:T(8,128)} %fusion), calls=%async_computation.1 | async-start | bytes 1048576 | tf_op jit(solution)/shard_map/all_to_all | solution.py:260
